TPU v7x, 32 devices: a whole 2x2x4 slice. The times are simulated.
32 devices in a mesh: slab: 2 (over x), py: 4 (over y, core), px: 4 (over z).
Axes of the slice: x: 2, y: 2, z: 4, core: 2. Of those that a mesh axis runs over, the one named last changes fastest.
Arguments:
- state: bfloat16 [2, 3, 16, 1024, 1024], P(None, None, 'slab', ('py', 'px')), may hold values from -12 to 12
- shells: int32 [16, 1024, 1024], P('slab', ('py', 'px')), may hold values from 0 to 511
Outputs:
- restored: float32 [2, 3, 16, 1024, 1024], P(None, None, ('slab', 'py'), None, 'px')
- spectrum: float32 [512], replicated
All inputs are finite; a program needn't handle non-finite values.
Results may differ from a plain program's by a relative error of at most 0.0003.
Values may be sent and summed in bfloat16 or wider, within the bound.
A program may use at most 128 MiB of HBM per device.

v0:
```python
import math
import jax
import jax.numpy as jnp
from jax import lax
from jax.sharding import PartitionSpec as P

SHELLS = 512


def mode_energy(values):
    return 0.5 * jnp.sum(values * values, axis=(0, 1))


def bin_energy(energy, labels_in):
    flat_energy = energy.reshape(-1)
    flat_labels = labels_in.reshape(-1)
    mode_count = flat_energy.shape[0]
    block_len = math.gcd(mode_count, 16384)
    high_rows = SHELLS // 128
    energy_blocks = flat_energy.reshape(mode_count // block_len, block_len)
    label_blocks = flat_labels.reshape(mode_count // block_len, block_len)

    def add_block(running, pieces):
        values, labels = pieces
        upper = values.astype(jnp.bfloat16)
        remain = values - upper.astype(jnp.float32)
        middle = remain.astype(jnp.bfloat16)
        lower = (remain - middle.astype(jnp.float32)).astype(jnp.bfloat16)
        high_part = labels // 128
        low_part = labels % 128
        high_hot = (high_part[:, None] == jnp.arange(high_rows, dtype=jnp.int32)[None, :]).astype(
            jnp.bfloat16
        )
        weighted = jnp.concatenate(
            [high_hot * upper[:, None], high_hot * middle[:, None], high_hot * lower[:, None]],
            axis=1,
        )
        onehot = (low_part[:, None] == jnp.arange(128, dtype=jnp.int32)[None, :]).astype(
            jnp.bfloat16
        )
        partial_sum = lax.dot_general(
            weighted, onehot, (((0,), (0,)), ((), ())), preferred_element_type=jnp.float32
        )
        partial_sum = partial_sum.reshape(3, high_rows, 128)
        return (running + (partial_sum[0] + partial_sum[1] + partial_sum[2]), None)

    running, _ = lax.scan(
        add_block, jnp.zeros((high_rows, 128), jnp.float32), (energy_blocks, label_blocks)
    )
    return running.reshape(SHELLS)


def local(state, shells):
    py_count = lax.axis_size("py")
    px_count = lax.axis_size("px")
    planes = state.shape[2]
    rows_local = state.shape[3]
    columns = state.shape[4]
    planes_out = planes // py_count
    columns_out = columns // px_count
    sectioned = state.reshape(2, 3, planes, 1, 1, rows_local, columns)
    received = lax.all_to_all(
        lax.all_to_all(sectioned, "py", split_axis=2, concat_axis=3, tiled=True),
        "px",
        split_axis=6,
        concat_axis=4,
        tiled=True,
    )
    restored = received.reshape(
        2, 3, planes_out, rows_local * py_count * px_count, columns_out
    ).astype(jnp.float32)
    totals = bin_energy(mode_energy(state.astype(jnp.float32)), shells)
    modes_all = planes * rows_local * columns * lax.axis_size("slab") * py_count * px_count
    totals = lax.psum(totals, ("slab", "py", "px"))
    spectrum = totals * (SHELLS / modes_all)
    return (restored, spectrum)


def solution(mesh):
    return jax.shard_map(
        local,
        mesh=mesh,
        in_specs=(P(None, None, "slab", ("py", "px"), None), P("slab", ("py", "px"), None)),
        out_specs=(P(None, None, ("slab", "py"), None, "px"), P()),
        check_vma=False,
    )
```

profile of v0, /device:TPU:0, one launch (start us, length us, event | category | flops | bytes accessed | tf_op | source)
XLA Modules:
  0.0 352.4 jit_solution(16731340654529815363)
XLA Ops:
  0.6 6.7 %copy.16 = bf16[2,3,8,64,1024]{4,3,1,0,2:T(8,128)(2,1)} copy(bf16[2,3,8,64,1024]{4,3,2,1,0:T(8,128)(2,1)} %param.4) | data formatting | bytes 12582912 | tf_op args[0]
  7.4 5.3 %all-to-all-start = ((bf16[2,3,8,1,1,64,1024]{6,5,1,0,4,3,2:T(8,128)(2,1)}), bf16[2,3,8,1,1,64,1024]{6,5,1,0,4,3,2:T(8,128)(2,1)}, u32[]{:S(2)}, u32[]{:S(2)}) async-start(bf16[2,3,8,1,1,64,1024]{6,5,1,0,4,3,2:T(8,128)(2,1)} %bitcast.24), calls=%async_computation | async-start | bytes 12582912 | tf_op jit(solution)/shard_map/all_to_all | solution.py:63
  12.6 4.6 %multiply_reduce_fusion = f32[8,64,1024]{2,1,0:T(8,128)S(1)} fusion(bf16[2,3,8,64,1024]{4,3,2,1,0:T(8,128)(2,1)} %param.4), kind=kLoop, calls=%fused_computation.29 | loop fusion | flops 8912896 | bytes 8388608 | tf_op jit(solution)/shard_map/reduce_sum | solution.py:11
  20.7 63.3 %all-to-all-done = bf16[2,3,8,1,1,64,1024]{6,5,1,0,4,3,2:T(8,128)(2,1)} async-done(((bf16[2,3,8,1,1,64,1024]{6,5,1,0,4,3,2:T(8,128)(2,1)}), bf16[2,3,8,1,1,64,1024]{6,5,1,0,4,3,2:T(8,128)(2,1)}, u32[]{:S(2)}, u32[]{:S(2)}) %all-to-all-start) | async-done | bytes 6291488 | tf_op jit(solution)/shard_map/all_to_all | solution.py:63
  84.0 20.1 %copy.12 = bf16[2,3,4,2,1,1,64,1024]{6,2,3,1,0,7,5,4:T(4,128)(2,1)} copy(bf16[2,3,4,2,1,1,64,1024]{7,6,1,0,3,2,5,4:T(8,128)(2,1)} %bitcast.1) | data formatting | bytes 12582912 | tf_op jit(solution)/shard_map/all_to_all | solution.py:63
  104.1 10.9 %bitcast_bitcast_fusion = bf16[1024,1,2,3,2,4,64]{6,5,4,3,2,1,0:T(4,128)(2,1)} fusion(bf16[2,3,4,2,1,1,64,1024]{6,2,3,1,0,7,5,4:T(4,128)(2,1)} %copy.12), kind=kLoop, calls=%fused_computation.33 | loop fusion | bytes 12582912
  115.0 12.8 %reshape.115 = bf16[4,2,393216]{2,1,0:T(2,128)(2,1)} reshape(bf16[1024,1,2,3,2,4,64]{6,5,4,3,2,1,0:T(4,128)(2,1)} %bitcast_bitcast_fusion) | data formatting | bytes 12582912
  127.8 5.7 %all-to-all-start.1 = ((bf16[4,2,393216]{2,1,0:T(2,128)(2,1)}), bf16[4,2,393216]{2,1,0:T(2,128)(2,1)}, u32[]{:S(2)}, u32[]{:S(2)}) async-start(bf16[4,2,393216]{2,1,0:T(2,128)(2,1)} %reshape.115), calls=%async_computation.1 | async-start | bytes 12582912 | tf_op jit(solution)/shard_map/all_to_all | solution.py:62
  133.5 122.2 %while.13 = (s32[]{:T(128)}, f32[4,128]{1,0:T(4,128)S(1)}, s32[32,16384]{1,0:T(8,128)S(1)}, f32[32,16384]{1,0:T(8,128)}, s32[]{:T(128)}, /*index=5*/s32[]{:T(128)}) while((s32[]{:T(128)}, f32[4,128]{1,0:T(4,128)S(1)}, s32[32,16384]{1,0:T(8,128)S(1)}, f32[32,16384]{1,0:T(8,128)}, s32[]{:T(128)}, /*index=5*/s32[]{:T(128)}) %tuple.44), condition=%wide.region_2.3_spmd.clone, body=%wide.region_1.2_spmd.clone.sunk | while | flops 54315008 | bytes 1720407 | solution.py:47
  138.8 2.3 fusion.23
  142.6 2.3 fusion.23
  150.2 2.3 fusion.23
  154.0 2.3 fusion.23
  161.7 2.3 fusion.23
  165.5 2.3 fusion.23
  173.1 2.3 fusion.23
  176.9 2.3 fusion.23
  184.6 2.3 fusion.23
  188.4 2.3 fusion.23
  255.7 40.2 %psum.7 = f32[512]{0:T(512)S(1)} all-reduce(f32[512]{0:T(512)S(1)} %bitcast.29), channel_id=1, replica_groups=mesh['slab'=2,'py'=4,'px'=4] {'slab','py','px'}, use_global_device_ids=true, to_apply=%region_3.4 | all-reduce | flops 512 | bytes 4096 | tf_op jit(solution)/shard_map/psum | solution.py:74
  296.5 12.7 %reshape.116 = bf16[1024,1,2,3,2,4,64]{6,5,4,3,2,1,0:T(4,128)(2,1)} reshape(bf16[4,2,393216]{2,1,0:T(2,128)(2,1)} %all-to-all-done.1) | data formatting | bytes 12582912
  309.2 18.5 %copy.13 = bf16[2,3,2,4,1,64,1024]{6,5,4,3,2,1,0:T(8,128)(2,1)} copy(bf16[2,3,2,4,1,64,1024]{5,3,2,1,0,4,6:T(4,128)(2,1)} %bitcast.22) | data formatting | bytes 12582912 | tf_op jit(solution)/shard_map/all_to_all | solution.py:62
  327.7 12.6 %reshape.114 = f32[2,3,2,4,1,64,4,256]{7,6,5,3,2,1,0,4:T(4,128)} reshape(bf16[2,3,2,4,1,64,1024]{6,5,4,3,2,1,0:T(8,128)(2,1)} %copy.13) | data formatting | bytes 18874368 | tf_op jit(solution)/shard_map/convert_element_type | solution.py:71
  340.3 12.0 %copy.14 = f32[2,3,2,4,4,1,64,256]{7,6,4,3,2,1,0,5:T(8,128)} copy(f32[2,3,2,4,4,1,64,256]{7,4,6,3,2,1,0,5:T(4,128)} %bitcast.23) | data formatting | bytes 25165824 | tf_op jit(solution)/shard_map/convert_element_type | solution.py:71
  (252 shorter events, 100.9 us)
Async XLA Ops:
  7.4 76.6 %all-to-all-start = ((bf16[2,3,8,1,1,64,1024]{6,5,1,0,4,3,2:T(8,128)(2,1)}), bf16[2,3,8,1,1,64,1024]{6,5,1,0,4,3,2:T(8,128)(2,1)}, u32[]{:S(2)}, u32[]{:S(2)}) async-start(bf16[2,3,8,1,1,64,1024]{6,5,1,0,4,3,2:T(8,128)(2,1)} %bitcast.24), calls=%async_computation | async-start | bytes 12582912 | tf_op jit(solution)/shard_map/all_to_all | solution.py:63
  127.8 168.7 %all-to-all-start.1 = ((bf16[4,2,393216]{2,1,0:T(2,128)(2,1)}), bf16[4,2,393216]{2,1,0:T(2,128)(2,1)}, u32[]{:S(2)}, u32[]{:S(2)}) async-start(bf16[4,2,393216]{2,1,0:T(2,128)(2,1)} %reshape.115), calls=%async_computation.1 | async-start | bytes 12582912 | tf_op jit(solution)/shard_map/all_to_all | solution.py:62
where the time goes:
time: 356 us; the launch traced here: 352 us
  local copies, waits for them, and re-layouts  146 us (41%)
  matrix products  74.9 us (21%)
  waiting for transfers between devices  63.3 us (18%)
  blocking collectives  40.2 us (11%)
  other arithmetic  14 us (4%)
  starting transfers between devices  10.9 us (3%)
    dot_general x32, matrix products, add_block(): lax.dot_general(weighted, onehot, (((0,), (0,)), ((), ())), preferred_ele...  74.9 us
    all_to_all x1, waiting for transfers between devices, local(): lax.all_to_all(sectioned, 'py', split_axis=2, concat_axis=3, tiled=True)  63.3 us
    unnamed x4, local copies, waits for them, and re-layouts  43.1 us
    psum x1, blocking collectives, local(): totals = lax.psum(totals, ('slab', 'py', 'px'))  40.2 us
    dynamic_slice x64, local copies, waits for them, and re-layouts, bin_energy(): lax.scan(add_block, jnp.zeros((high_rows, 128), jnp.float32), (energy_blo...  36.7 us
    convert_element_type x2, local copies, waits for them, and re-layouts, local(): restored = received.reshape(2, 3, planes_out, rows_local * py_count * px_...  24.7 us
    all_to_all x1, local copies, waits for them, and re-layouts, local(): lax.all_to_all(sectioned, 'py', split_axis=2, concat_axis=3, tiled=True)  20.1 us
    all_to_all x1, local copies, waits for them, and re-layouts, local(): lax.all_to_all(lax.all_to_all(sectioned, 'py', split_axis=2, concat_axis=...  18.5 us
  transfers between devices with their start and end apart: 2, of which 1 were waited for; matrix products, arithmetic and copies ran while one was open for 37% of the time, Pallas kernels for 0%

commit v1 on v0

--- a/solution.py
+++ b/solution.py
@@ -59,12 +59,20 @@
     planes_out = planes // py_count
     columns_out = columns // px_count
     sectioned = state.reshape(2, 3, planes, 1, 1, rows_local, columns)
-    received = lax.all_to_all(
-        lax.all_to_all(sectioned, "py", split_axis=2, concat_axis=3, tiled=True),
-        "px",
-        split_axis=6,
-        concat_axis=4,
-        tiled=True,
+    received = jnp.concatenate(
+        lax.all_to_all(
+            jnp.stack(
+                jnp.split(
+                    lax.all_to_all(sectioned, "py", split_axis=2, concat_axis=3, tiled=True),
+                    lax.axis_size("px"),
+                    axis=6,
+                )
+            ),
+            "px",
+            0,
+            0,
+        ),
+        axis=4,
     )
     restored = received.reshape(
         2, 3, planes_out, rows_local * py_count * px_count, columns_out

time: 356 us -> 271 us (0.76)
  local copies, waits for them, and re-layouts: 146 us -> 51.2 us
  other arithmetic: 14 us -> 26.3 us
    unnamed x4 -> x1, local copies, waits for them, and re-layouts: 43.1 us -> 6.74 us
    convert_element_type x2 -> x0, local copies, waits for them, and re-layouts: 24.7 us -> none  [local(): restored = received.reshape(2, 3, planes_out, rows_local * py_count * px_...]
    all_to_all x1 -> x0, local copies, waits for them, and re-layouts: 18.5 us -> none  [local(): lax.all_to_all(lax.all_to_all(sectioned, 'py', split_axis=2, concat_axis=...]
    all_to_all x1, local copies, waits for them, and re-layouts: 20.1 us -> 3.49 us  [local(): lax.all_to_all(sectioned, 'py', split_axis=2, concat_axis=3, tiled=True)]
    convert_element_type x0 -> x1, other arithmetic: none -> 9.13 us  [local(): restored = received.reshape(2, 3, planes_out, rows_local * py_count * px_...]
  transfers between devices with their start and end apart: 2 -> 2, of which waited for: 1 -> 1; matrix products, arithmetic and copies ran while one was open for 37% -> 48% of each run, Pallas kernels for 0% -> 0%
where the time goes in v1:
time: 271 us; the launch traced here: 269 us
  matrix products  74.9 us (28%)
  waiting for transfers between devices  63.3 us (23%)
  local copies, waits for them, and re-layouts  51.2 us (19%)
  blocking collectives  40 us (15%)
  other arithmetic  26.3 us (10%)
  starting transfers between devices  10.9 us (4%)
    dot_general x32, matrix products, add_block(): lax.dot_general(weighted, onehot, (((0,), (0,)), ((), ())), preferred_ele...  74.9 us
    all_to_all x1, waiting for transfers between devices, local(): lax.all_to_all(sectioned, 'py', split_axis=2, concat_axis=3, tiled=True)  63.3 us
    psum x1, blocking collectives, local(): totals = lax.psum(totals, ('slab', 'py', 'px'))  40 us
    dynamic_slice x64, local copies, waits for them, and re-layouts, bin_energy(): lax.scan(add_block, jnp.zeros((high_rows, 128), jnp.float32), (energy_blo...  36.7 us
    convert_element_type x1, other arithmetic, local(): restored = received.reshape(2, 3, planes_out, rows_local * py_count * px_...  9.13 us
    unnamed x1, local copies, waits for them, and re-layouts  6.74 us
    all_to_all x1, starting transfers between devices, local(): lax.all_to_all(jnp.stack(jnp.split(lax.all_to_all(sectioned, 'py', split_...  5.67 us
    mul x32, other arithmetic, add_block(): high_hot * upper[:, None]  5.57 us
  transfers between devices with their start and end apart: 2, of which 1 were waited for; matrix products, arithmetic and copies ran while one was open for 48% of the time, Pallas kernels for 0%

profile of v1, /device:TPU:0, one launch (start us, length us, event | category | flops | bytes accessed | tf_op | source)
XLA Modules:
  0.0 269.2 jit_solution(14379471272853002307)
XLA Ops:
  0.6 6.7 %copy.17 = bf16[2,3,8,64,1024]{4,3,1,0,2:T(8,128)(2,1)} copy(bf16[2,3,8,64,1024]{4,3,2,1,0:T(8,128)(2,1)} %param.4) | data formatting | bytes 12582912 | tf_op args[0]
  7.4 5.3 %all-to-all-start = ((bf16[2,3,8,1,1,64,1024]{6,5,1,0,4,3,2:T(8,128)(2,1)}), bf16[2,3,8,1,1,64,1024]{6,5,1,0,4,3,2:T(8,128)(2,1)}, u32[]{:S(2)}, u32[]{:S(2)}) async-start(bf16[2,3,8,1,1,64,1024]{6,5,1,0,4,3,2:T(8,128)(2,1)} %bitcast.27), calls=%async_computation | async-start | bytes 12582912 | tf_op jit(solution)/shard_map/all_to_all | solution.py:66
  12.6 4.6 %multiply_reduce_fusion = f32[8,64,1024]{2,1,0:T(8,128)S(1)} fusion(bf16[2,3,8,64,1024]{4,3,2,1,0:T(8,128)(2,1)} %param.4), kind=kLoop, calls=%fused_computation.29 | loop fusion | flops 8912896 | bytes 8388608 | tf_op jit(solution)/shard_map/reduce_sum | solution.py:11
  20.7 63.3 %all-to-all-done = bf16[2,3,8,1,1,64,1024]{6,5,1,0,4,3,2:T(8,128)(2,1)} async-done(((bf16[2,3,8,1,1,64,1024]{6,5,1,0,4,3,2:T(8,128)(2,1)}), bf16[2,3,8,1,1,64,1024]{6,5,1,0,4,3,2:T(8,128)(2,1)}, u32[]{:S(2)}, u32[]{:S(2)}) %all-to-all-start) | async-done | bytes 6291488 | tf_op jit(solution)/shard_map/all_to_all | solution.py:66
  84.0 3.5 %copy.16 = bf16[2,3,4,2,1,1,64,1024]{7,6,2,3,1,0,5,4:T(8,128)(2,1)S(1)} copy(bf16[2,3,4,2,1,1,64,1024]{7,6,1,0,3,2,5,4:T(8,128)(2,1)} %bitcast.1) | data formatting | bytes 12582912 | tf_op jit(solution)/shard_map/all_to_all | solution.py:66
  88.4 3.2 %pad_maximum_fusion = bf16[4,2,3,2,4,1,64,256]{7,6,4,3,2,1,5,0:T(8,128)(2,1)} fusion(bf16[1,2,3,2,4,1,64,256]{7,6,4,3,2,1,5,0:T(8,128)(2,1)S(1)} %get-tuple-element.90, bf16[1,2,3,2,4,1,64,256]{7,6,4,3,2,1,5,0:T(8,128)(2,1)S(1)} %get-tuple-element.91, bf16[1,2,3,2,4,1,64,256]{7,6,4,3,2,1,5,0:T(8,128)(2,1)S(1)} %get-tuple-element.92, ...), kind=kLoop, calls=%fused_computation.30 | loop fusion | flops 9437184 | bytes 12582912 | tf_op jit(solution)/shard_map/stack | solution.py:64
  91.5 5.7 %all-to-all-start.1 = ((bf16[4,2,3,2,4,1,64,256]{7,6,4,3,2,1,5,0:T(8,128)(2,1)}), bf16[4,2,3,2,4,1,64,256]{7,6,4,3,2,1,5,0:T(8,128)(2,1)}, u32[]{:S(2)}, u32[]{:S(2)}) async-start(bf16[4,2,3,2,4,1,64,256]{7,6,4,3,2,1,5,0:T(8,128)(2,1)} %pad_maximum_fusion), calls=%async_computation.1 | async-start | bytes 12582912 | tf_op jit(solution)/shard_map/all_to_all | solution.py:63
  97.2 122.2 %while.13 = (s32[]{:T(128)}, f32[4,128]{1,0:T(4,128)S(1)}, s32[32,16384]{1,0:T(8,128)S(1)}, f32[32,16384]{1,0:T(8,128)}, s32[]{:T(128)}, /*index=5*/s32[]{:T(128)}) while((s32[]{:T(128)}, f32[4,128]{1,0:T(4,128)S(1)}, s32[32,16384]{1,0:T(8,128)S(1)}, f32[32,16384]{1,0:T(8,128)}, s32[]{:T(128)}, /*index=5*/s32[]{:T(128)}) %tuple.47), condition=%wide.region_2.3_spmd.clone, body=%wide.region_1.2_spmd.clone.sunk | while | flops 54315008 | bytes 1720407 | solution.py:47
  98.7 2.3 fusion.23
  102.5 2.3 fusion.23
  110.1 2.3 fusion.23
  113.9 2.3 fusion.23
  121.6 2.3 fusion.23
  125.4 2.3 fusion.23
  133.0 2.3 fusion.23
  136.8 2.3 fusion.23
  148.3 2.3 fusion.23
  152.1 2.3 fusion.23
  159.8 2.3 fusion.23
  163.6 2.3 fusion.23
  171.2 2.3 fusion.23
  175.0 2.3 fusion.23
  219.4 40.0 %psum.7 = f32[512]{0:T(512)S(1)} all-reduce(f32[512]{0:T(512)S(1)} %bitcast.33), channel_id=1, replica_groups=mesh['slab'=2,'py'=4,'px'=4] {'slab','py','px'}, use_global_device_ids=true, to_apply=%region_3.4 | all-reduce | flops 512 | bytes 4096 | tf_op jit(solution)/shard_map/psum | solution.py:82
  260.1 9.1 %copy_convert_fusion = f32[4,2,3,2,4,1,64,256]{7,6,0,4,3,2,1,5:T(8,128)} fusion(bf16[4,2,3,2,4,1,64,256]{7,6,4,3,2,1,5,0:T(8,128)(2,1)} %all-to-all-done.1), kind=kLoop, calls=%fused_computation.31 | loop fusion | flops 3145728 | bytes 18874368 | tf_op jit(solution)/shard_map/convert_element_type | solution.py:79
  (249 shorter events, 92.4 us)
Async XLA Ops:
  7.4 76.6 %all-to-all-start = ((bf16[2,3,8,1,1,64,1024]{6,5,1,0,4,3,2:T(8,128)(2,1)}), bf16[2,3,8,1,1,64,1024]{6,5,1,0,4,3,2:T(8,128)(2,1)}, u32[]{:S(2)}, u32[]{:S(2)}) async-start(bf16[2,3,8,1,1,64,1024]{6,5,1,0,4,3,2:T(8,128)(2,1)} %bitcast.27), calls=%async_computation | async-start | bytes 12582912 | tf_op jit(solution)/shard_map/all_to_all | solution.py:66
  91.5 168.5 %all-to-all-start.1 = ((bf16[4,2,3,2,4,1,64,256]{7,6,4,3,2,1,5,0:T(8,128)(2,1)}), bf16[4,2,3,2,4,1,64,256]{7,6,4,3,2,1,5,0:T(8,128)(2,1)}, u32[]{:S(2)}, u32[]{:S(2)}) async-start(bf16[4,2,3,2,4,1,64,256]{7,6,4,3,2,1,5,0:T(8,128)(2,1)} %pad_maximum_fusion), calls=%async_computation.1 | async-start | bytes 12582912 | tf_op jit(solution)/shard_map/all_to_all | solution.py:63
